TPU v7x, 32 devices: a whole 2x2x4 slice. The times are simulated.
32 devices in a mesh: dp: 2 (over x), fsdp: 4 (over z), mp: 4 (over y, core).
Axes of the slice: x: 2, y: 2, z: 4, core: 2. Of those that a mesh axis runs over, the one named last changes fastest.
Arguments:
- gradients: bfloat16 [8, 12, 2, 256, 1024], P(('dp', 'fsdp'), None, None, None, 'mp'), may hold values from -6 to 6
- master: float32 [12, 2, 256, 1024], P(None, None, ('dp', 'fsdp'), 'mp'), may hold values from -0.375 to 0.375
- teacher: float32 [12, 2, 256, 1024], P(None, None, ('dp', 'fsdp'), 'mp'), may hold values from -0.375 to 0.375
- first_moment: float32 [12, 2, 256, 1024], P(None, None, ('dp', 'fsdp'), 'mp'), may hold values from -2.2888184e-05 to 2.2888184e-05
- second_moment: float32 [12, 2, 256, 1024], P(None, None, ('dp', 'fsdp'), 'mp'), may hold values from 0 to 1, as said below
- layer_rates: float32 [12], replicated, may hold values from 0.02 to 0.2
Outputs:
- master_new: float32 [12, 2, 256, 1024], P(None, None, ('dp', 'fsdp'), 'mp')
- teacher_new: float32 [12, 2, 256, 1024], P(None, None, ('dp', 'fsdp'), 'mp')
- first_new: float32 [12, 2, 256, 1024], P(None, None, ('dp', 'fsdp'), 'mp')
- second_new: float32 [12, 2, 256, 1024], P(None, None, ('dp', 'fsdp'), 'mp')
- student_weights: bfloat16 [12, 2, 256, 1024], P(None, None, None, 'mp')
- teacher_weights: bfloat16 [12, 2, 256, 1024], P(None, None, None, 'mp')
Inputs may be any that keep to these rules, and one draw needn't show every extreme that they name: `second_moment`: every entry is positive.
All inputs are finite; a program needn't handle non-finite values.
Results may differ from a plain program's by a relative error of at most 0.0004.
Values may be sent and summed in bfloat16 or wider, within the bound.
A program may use at most 64 MiB of HBM per device.

v0:
```python
import jax
import jax.numpy as jnp
from jax import lax
from jax.sharding import PartitionSpec as P

CLIP_NORM = 0.1
BETA_ONE = 0.9
BETA_TWO = 0.999
BIAS_ONE = 1.0 - 0.9**50 * 0.9**50
BIAS_TWO = 1.0 - 0.999**50 * 0.999**50
ADAM_EPS = 1e-08
DECAY = 0.05
EMA_KEEP = 0.95


def shards(gradients, master, teacher, first_moment, second_moment, layer_rates):
    own_grad = gradients[0].astype(jnp.float32)
    summed = lax.psum_scatter(own_grad, ("dp", "fsdp"), scatter_dimension=2, tiled=True)
    mean_grad = summed / (lax.axis_size("dp") * lax.axis_size("fsdp"))
    norm_sq = lax.psum(jnp.sum(mean_grad * mean_grad), ("dp", "fsdp", "mp"))
    clip_factor = jnp.minimum(1.0, CLIP_NORM / (jnp.sqrt(norm_sq) + 1e-06))
    clipped = clip_factor * mean_grad
    first_new = BETA_ONE * first_moment + (1.0 - BETA_ONE) * clipped
    second_new = BETA_TWO * second_moment + (1.0 - BETA_TWO) * clipped * clipped
    direction = first_new / BIAS_ONE / (jnp.sqrt(second_new / BIAS_TWO) + ADAM_EPS) + DECAY * master
    layer_rate = layer_rates[:, None, None, None]
    master_new = master - layer_rate * direction
    teacher_new = EMA_KEEP * teacher + (1.0 - EMA_KEEP) * master_new
    student_half = master_new.astype(jnp.bfloat16)
    teacher_half = teacher_new.astype(jnp.bfloat16)
    student_weights, teacher_weights = (
        lax.all_gather(student_half, ("dp", "fsdp"), axis=2, tiled=True),
        lax.all_gather(teacher_half, ("dp", "fsdp"), axis=2, tiled=True),
    )
    return (master_new, teacher_new, first_new, second_new, student_weights, teacher_weights)


def solution(mesh):
    placed = (
        P(("dp", "fsdp"), None, None, None, "mp"),
        P(None, None, ("dp", "fsdp"), "mp"),
        P(None, None, ("dp", "fsdp"), "mp"),
        P(None, None, ("dp", "fsdp"), "mp"),
        P(None, None, ("dp", "fsdp"), "mp"),
        P(),
    )
    return jax.shard_map(
        shards,
        mesh=mesh,
        in_specs=placed,
        out_specs=(
            P(None, None, ("dp", "fsdp"), "mp"),
            P(None, None, ("dp", "fsdp"), "mp"),
            P(None, None, ("dp", "fsdp"), "mp"),
            P(None, None, ("dp", "fsdp"), "mp"),
            P(None, None, None, "mp"),
            P(None, None, None, "mp"),
        ),
        check_vma=False,
    )
```

profile of v0, /device:TPU:0, one launch (start us, length us, event | category | flops | bytes accessed | tf_op | source)
XLA Modules:
  0.0 313.6 jit_solution(9749156798036131048)
XLA Ops:
  7.2 0.0 reduce-scatter.2.cloned.1.call-start
  7.2 5.3 %bitcast_convert_fusion = f32[12,2,256,256]{3,2,1,0:T(8,128)} fusion(bf16[1,12,2,256,256]{4,3,2,1,0:T(8,128)(2,1)} %param.6), kind=kLoop, calls=%fused_computation | loop fusion | flops 1572864 | bytes 9437184 | tf_op jit(solution)/shard_map/convert_element_type | solution.py:17
  12.5 0.0 copy-start.2
  12.5 0.0 copy-start.3
  12.5 0.0 copy-start.4
  12.5 0.0 copy-start.5
  12.5 0.0 reduce-scatter.2.cloned.1.call-update
  12.6 0.0 all-gather.5.cloned.1.call-start
  12.6 121.3 %reduce-scatter.2.cloned.1.call-done = f32[12,2,32,256]{3,2,1,0:T(8,128)} async-done(((f32[12,2,256,256]{3,2,1,0:T(8,128)}), f32[12,2,32,256]{3,2,1,0:T(8,128)}) %reduce-scatter.2.cloned.1.call-update) | async-done | bytes 786448 | tf_op jit(solution)/shard_map/reduce_scatter | solution.py:18
  133.9 1.9 multiply_reduce_fusion
  135.8 39.7 %psum.7 = f32[]{:T(128)} all-reduce(f32[]{:T(128)} %multiply_reduce_fusion), channel_id=1, replica_groups=mesh['dp'=2,'fsdp'=4,'mp'=4] {'dp','fsdp','mp'}, use_global_device_ids=true, to_apply=%region_2.0 | all-reduce | flops 1 | bytes 8 | tf_op jit(solution)/shard_map/psum | solution.py:20
  176.3 0.0 copy-done.2
  176.3 0.0 copy-done.3
  176.3 0.0 copy-done.4
  176.3 0.0 copy-done.5
  176.3 3.5 %fusion.1 = (bf16[12,2,32,256]{3,2,1,0:T(8,128)(2,1)}, f32[12,2,32,256]{3,2,1,0:T(8,128)}, f32[12,2,32,256]{3,2,1,0:T(8,128)S(1)}, f32[12,2,32,256]{3,2,1,0:T(8,128)}, f32[12,2,32,256]{3,2,1,0:T(8,128)}) fusion(f32[12,2,32,256]{3,2,1,0:T(8,128)S(1)} %copy-done.2, f32[12,2,32,256]{3,2,1,0:T(8,128)S(1)} %copy-done.3, f32[12]{0:T(128)S(1)} %copy-done.5, ...), kind=kLoop, calls=%fused_computation.7 | loop fusion | flops 3932160 | bytes 7471156 | tf_op jit(solution)/shard_map/convert_element_type | solution.py:30
  179.8 0.0 copy-start.1
  179.8 0.0 all-gather.5.cloned.1.call-update
  179.8 0.0 all-gather.3.cloned.1.call-start
  179.9 1.0 convert_element_type.14
  180.9 0.0 all-gather.3.cloned.1.call-update
  180.9 59.0 %all-gather.5.cloned.1.call-done = bf16[12,2,256,256]{3,2,1,0:T(8,128)(2,1)} async-done(((bf16[12,2,32,256]{3,2,1,0:T(8,128)(2,1)}), bf16[12,2,256,256]{3,2,1,0:T(8,128)(2,1)}) %all-gather.5.cloned.1.call-update) | async-done | bytes 3145744 | tf_op jit(solution)/shard_map/all_gather | solution.py:33
  239.9 61.5 %all-gather.3.cloned.1.call-done = bf16[12,2,256,256]{3,2,1,0:T(8,128)(2,1)} async-done(((bf16[12,2,32,256]{3,2,1,0:T(8,128)(2,1)}), bf16[12,2,256,256]{3,2,1,0:T(8,128)(2,1)}) %all-gather.3.cloned.1.call-update) | async-done | bytes 3145744 | tf_op jit(solution)/shard_map/all_gather | solution.py:32
  301.4 0.0 copy-start
  301.4 4.0 %copy.14 = bf16[12,2,256,256]{3,2,1,0:T(8,128)(2,1)} copy(bf16[12,2,256,256]{3,2,1,0:T(8,128)(2,1)} %all-gather.3.cloned.1.call-done) | data formatting | bytes 6291456
  305.4 0.0 copy-done.1
  305.4 0.0 copy-done
  305.4 1.7 copy.15
Async XLA Ops:
  7.2 126.7 %reduce-scatter.2.cloned.1.call-start = ((), (), s32[]{:S(2)}) async-start(), calls=%async_computation.1 | async-start | bytes 7077888 | tf_op jit(solution)/shard_map/reduce_scatter | solution.py:18
  12.5 163.8 %copy-start.2 = (f32[12,2,32,256]{3,2,1,0:T(8,128)S(1)}, f32[12,2,32,256]{3,2,1,0:T(8,128)}, u32[]{:S(2)}) copy-start(f32[12,2,32,256]{3,2,1,0:T(8,128)} %param.8) | copy-start | bytes 2359300
  12.5 163.8 %copy-start.3 = (f32[12,2,32,256]{3,2,1,0:T(8,128)S(1)}, f32[12,2,32,256]{3,2,1,0:T(8,128)}, u32[]{:S(2)}) copy-start(f32[12,2,32,256]{3,2,1,0:T(8,128)} %param.7) | copy-start | bytes 2359300
  12.5 163.8 %copy-start.4 = (f32[12,2,32,256]{3,2,1,0:T(8,128)S(1)}, f32[12,2,32,256]{3,2,1,0:T(8,128)}, u32[]{:S(2)}) copy-start(f32[12,2,32,256]{3,2,1,0:T(8,128)} %param.9) | copy-start | bytes 2359300
  12.5 163.8 %copy-start.5 = (f32[12]{0:T(128)S(1)}, f32[12]{0:T(128)}, u32[]{:S(2)}) copy-start(f32[12]{0:T(128)} %param.11) | copy-start | bytes 148
  12.6 227.4 %all-gather.5.cloned.1.call-start = ((), (), s32[]{:S(2)}) async-start(), calls=%async_computation.3 | async-start | bytes 3538944 | tf_op jit(solution)/shard_map/all_gather | solution.py:33
  179.8 125.6 %copy-start.1 = (f32[12,2,32,256]{3,2,1,0:T(8,128)}, f32[12,2,32,256]{3,2,1,0:T(8,128)S(1)}, u32[]{:S(2)}) copy-start(f32[12,2,32,256]{3,2,1,0:T(8,128)S(1)} %get-tuple-element.17) | copy-start | bytes 2359300
  179.8 121.6 %all-gather.3.cloned.1.call-start = ((), (), s32[]{:S(2)}) async-start(), calls=%async_computation.2 | async-start | bytes 3538944 | tf_op jit(solution)/shard_map/all_gather | solution.py:32
  301.4 4.0 %copy-start = (bf16[12,2,256,256]{3,2,1,0:T(8,128)(2,1)S(1)}, bf16[12,2,256,256]{3,2,1,0:T(8,128)(2,1)}, u32[]{:S(2)}) copy-start(bf16[12,2,256,256]{3,2,1,0:T(8,128)(2,1)} %all-gather.5.cloned.1.call-done) | copy-start | bytes 9437188
Sparse Core Ops, SparseCore 0:
  12.7 121.1 reduce-scatter.1
  180.0 59.9 all-gather.4
  242.7 58.6 all-gather.2
where the time goes:
time: 314 us
  waiting for transfers between devices  242 us (77%)
  blocking collectives  39.7 us (13%)
  between operations  14.5 us (5%)
  other arithmetic  11.7 us (4%)
  local copies, waits for them, and re-layouts  5.69 us (2%)
    reduce_scatter x1, waiting for transfers between devices, shards(): lax.psum_scatter(own_grad, ('dp', 'fsdp'), scatter_dimension=2, tiled=True)  121 us
    all_gather x1, waiting for transfers between devices, shards(): lax.all_gather(student_half, ('dp', 'fsdp'), axis=2, tiled=True)  61.5 us
    all_gather x1, waiting for transfers between devices, shards(): lax.all_gather(teacher_half, ('dp', 'fsdp'), axis=2, tiled=True)  59 us
    psum x1, blocking collectives, shards(): norm_sq = lax.psum(jnp.sum(mean_grad * mean_grad), ('dp', 'fsdp', 'mp'))  39.7 us
  transfers between devices with their start and end apart: 3, of which 3 were waited for; matrix products, arithmetic and copies ran while one was open for 0% of the time, Pallas kernels for 0%

commit v1 on v0

--- a/solution.py
+++ b/solution.py
@@ -1,3 +1,4 @@
+import functools
 import jax
 import jax.numpy as jnp
 from jax import lax
@@ -11,6 +12,28 @@
 ADAM_EPS = 1e-08
 DECAY = 0.05
 EMA_KEEP = 0.95
+
+
+def bars_begin(xs, axis_name):
+    all_values = lax.axis_index(axis_name)
+    plain = lax.axis_size(axis_name)
+    y2, small, odd = (plain, all_values, xs.shape[2])
+    samples = [(at, (at + 1) % y2) for at in range(y2)]
+    log = [(at, (at - 1) % y2) for at in range(y2)]
+    k_now = jnp.zeros((*xs.shape[:2], y2 * odd, *xs.shape[3:]), xs.dtype)
+    k_now = lax.dynamic_update_slice_in_dim(k_now, xs, small * odd, axis=2)
+    t1 = y2 // 2
+    fresh = s_next = xs
+    for ix in tuple(range(1, t1 + 1)):
+        fresh = lax.ppermute(fresh, axis_name, samples)
+        k_now = lax.dynamic_update_slice_in_dim(k_now, fresh, (small - ix) % y2 * odd, axis=2)
+        if ix < y2 - t1:
+            s_next = lax.ppermute(s_next, axis_name, log)
+            k_now = lax.dynamic_update_slice_in_dim(k_now, s_next, (small + ix) % y2 * odd, axis=2)
+    return k_now
+
+
+choose_slices = functools.partial(bars_begin, axis_name=("dp", "fsdp"))
 
 
 def shards(gradients, master, teacher, first_moment, second_moment, layer_rates):
@@ -29,7 +52,7 @@
     student_half = master_new.astype(jnp.bfloat16)
     teacher_half = teacher_new.astype(jnp.bfloat16)
     student_weights, teacher_weights = (
-        lax.all_gather(student_half, ("dp", "fsdp"), axis=2, tiled=True),
+        choose_slices(student_half),
         lax.all_gather(teacher_half, ("dp", "fsdp"), axis=2, tiled=True),
     )
     return (master_new, teacher_new, first_new, second_new, student_weights, teacher_weights)

time: 314 us -> 295 us (0.939)
  waiting for transfers between devices: 242 us -> 213 us
  starting transfers between devices: 0.12 us -> 5.72 us
  local copies, waits for them, and re-layouts: 5.69 us -> 10.3 us
    ppermute x0 -> x7, waiting for transfers between devices: none -> 91.6 us  [the longest x3 59.4 us: bars_begin(): s_next = lax.ppermute(s_next, axis_name, log)]
    all_gather x1 -> x0, waiting for transfers between devices: 61.5 us -> none  [shards(): lax.all_gather(student_half, ('dp', 'fsdp'), axis=2, tiled=True)]
    all_gather x1, waiting for transfers between devices: 59 us -> 0.02 us  [shards(): lax.all_gather(teacher_half, ('dp', 'fsdp'), axis=2, tiled=True)]
    ppermute x0 -> x7, starting transfers between devices: none -> 5.64 us  [the longest x3 3.66 us: bars_begin(): s_next = lax.ppermute(s_next, axis_name, log)]
    dynamic_update_slice x0 -> x7, local copies, waits for them, and re-layouts: none -> 4.21 us  [the longest x4 2.12 us: bars_begin(): lax.dynamic_update_slice_in_dim(k_now, fresh, (small - ix) % y2 * odd, ax...]
  transfers between devices with their start and end apart: 3 -> 9, of which waited for: 3 -> 8; matrix products, arithmetic and copies ran while one was open for 0% -> 2% of each run, Pallas kernels for 0% -> 0%
where the time goes in v1:
time: 295 us
  waiting for transfers between devices  213 us (72%)
  blocking collectives  39.7 us (13%)
  between operations  14.9 us (5%)
  other arithmetic  10.8 us (4%)
  local copies, waits for them, and re-layouts  10.3 us (3%)
  starting transfers between devices  5.72 us (2%)
    reduce_scatter x1, waiting for transfers between devices, shards(): lax.psum_scatter(own_grad, ('dp', 'fsdp'), scatter_dimension=2, tiled=True)  121 us
    ppermute x3, waiting for transfers between devices, bars_begin(): s_next = lax.ppermute(s_next, axis_name, log)  59.4 us
    psum x1, blocking collectives, shards(): norm_sq = lax.psum(jnp.sum(mean_grad * mean_grad), ('dp', 'fsdp', 'mp'))  39.7 us
    ppermute x4, waiting for transfers between devices, bars_begin(): fresh = lax.ppermute(fresh, axis_name, samples)  32.3 us
  transfers between devices with their start and end apart: 9, of which 8 were waited for; matrix products, arithmetic and copies ran while one was open for 2% of the time, Pallas kernels for 0%

profile of v1, /device:TPU:0, one launch (start us, length us, event | category | flops | bytes accessed | tf_op | source)
XLA Modules:
  0.0 294.5 jit_solution(7379937377530156153)
XLA Ops:
  7.2 0.0 reduce-scatter.2.cloned.1.call-start
  7.2 5.3 %bitcast_convert_fusion = f32[12,2,256,256]{3,2,1,0:T(8,128)} fusion(bf16[1,12,2,256,256]{4,3,2,1,0:T(8,128)(2,1)} %param.6), kind=kLoop, calls=%fused_computation | loop fusion | flops 1572864 | bytes 9437184 | tf_op jit(solution)/shard_map/convert_element_type | solution.py:40
  12.5 0.0 copy-start.2
  12.5 0.0 copy-start.3
  12.5 0.0 copy-start.4
  12.5 0.0 copy-start.5
  12.5 0.0 copy-start.7
  12.5 0.0 reduce-scatter.2.cloned.1.call-update
  12.6 0.0 all-gather.2.cloned.1.call-start
  12.6 121.3 %reduce-scatter.2.cloned.1.call-done = f32[12,2,32,256]{3,2,1,0:T(8,128)} async-done(((f32[12,2,256,256]{3,2,1,0:T(8,128)}), f32[12,2,32,256]{3,2,1,0:T(8,128)}) %reduce-scatter.2.cloned.1.call-update) | async-done | bytes 786448 | tf_op jit(solution)/shard_map/reduce_scatter | solution.py:41
  133.9 1.9 multiply_reduce_fusion
  135.8 39.7 %psum.7 = f32[]{:T(128)} all-reduce(f32[]{:T(128)} %multiply_reduce_fusion), channel_id=1, replica_groups=mesh['dp'=2,'fsdp'=4,'mp'=4] {'dp','fsdp','mp'}, use_global_device_ids=true, to_apply=%region_2.0 | all-reduce | flops 1 | bytes 8 | tf_op jit(solution)/shard_map/psum | solution.py:43
  176.3 0.0 copy-done.2
  176.3 0.0 copy-done.3
  176.3 0.0 copy-done.4
  176.3 0.0 copy-done.5
  176.3 0.0 copy-done.7
  176.3 3.5 %fusion.1 = (bf16[12,2,32,256]{3,2,1,0:T(8,128)(2,1)}, f32[12,2,32,256]{3,2,1,0:T(8,128)}, f32[12,2,32,256]{3,2,1,0:T(8,128)}, f32[12,2,32,256]{3,2,1,0:T(8,128)}, f32[12,2,32,256]{3,2,1,0:T(8,128)}) fusion(f32[12,2,32,256]{3,2,1,0:T(8,128)S(1)} %copy-done.2, f32[12,2,32,256]{3,2,1,0:T(8,128)S(1)} %copy-done.3, f32[12]{0:T(128)S(1)} %copy-done.7, ...), kind=kLoop, calls=%fused_computation.15 | loop fusion | flops 3932160 | bytes 7471156 | tf_op jit(solution)/shard_map/convert_element_type | solution.py:53
  179.9 0.0 all-gather.2.cloned.1.call-update
  179.9 0.0 copy-start.1
  179.9 0.3 broadcast_in_dim.4
  180.2 0.8 copy-done.1
  181.0 0.1 constant_dynamic-update-slice_fusion.7
  181.1 1.1 collective-permute-start
  182.2 3.7 %collective-permute-start.1 = (bf16[12,2,32,256]{3,2,1,0:T(8,128)(2,1)S(1)}, bf16[12,2,32,256]{3,2,1,0:T(8,128)(2,1)}, u32[]{:S(2)}, u32[]{:S(2)}) collective-permute-start(bf16[12,2,32,256]{3,2,1,0:T(8,128)(2,1)S(1)} %get-tuple-element.12), channel_id=1, source_target_pairs={{0,28},{4,0},{8,4},{12,8},{16,12},{20,16},{24,20},{28,24},{1,29},{... | collective-permute-start | bytes 1179656 | tf_op jit(solution)/shard_map/ppermute | solution.py:31
  185.9 12.2 %collective-permute-done = bf16[12,2,32,256]{3,2,1,0:T(8,128)(2,1)S(1)} collective-permute-done((bf16[12,2,32,256]{3,2,1,0:T(8,128)(2,1)S(1)}, bf16[12,2,32,256]{3,2,1,0:T(8,128)(2,1)S(1)}, u32[]{:S(2)}, u32[]{:S(2)}) %collective-permute-start) | collective-permute-done | bytes 393248 | tf_op jit(solution)/shard_map/ppermute | solution.py:28
  198.0 0.0 copy-start.6
  198.0 0.0 collective-permute-start.2
  198.1 19.4 %collective-permute-done.1 = bf16[12,2,32,256]{3,2,1,0:T(8,128)(2,1)} collective-permute-done((bf16[12,2,32,256]{3,2,1,0:T(8,128)(2,1)S(1)}, bf16[12,2,32,256]{3,2,1,0:T(8,128)(2,1)}, u32[]{:S(2)}, u32[]{:S(2)}) %collective-permute-start.1) | collective-permute-done | bytes 393248 | tf_op jit(solution)/shard_map/ppermute | solution.py:31
  217.4 0.0 collective-permute-start.3
  217.4 0.0 copy-done.6
  217.4 8.0 %collective-permute-done.2 = bf16[12,2,32,256]{3,2,1,0:T(8,128)(2,1)} collective-permute-done((bf16[12,2,32,256]{3,2,1,0:T(8,128)(2,1)S(1)}, bf16[12,2,32,256]{3,2,1,0:T(8,128)(2,1)}, u32[]{:S(2)}, u32[]{:S(2)}) %collective-permute-start.2) | collective-permute-done | bytes 393248 | tf_op jit(solution)/shard_map/ppermute | solution.py:28
  225.5 0.0 collective-permute-start.4
  225.5 1.0 constant_dynamic-update-slice_fusion.6
  226.5 24.8 %collective-permute-done.3 = bf16[12,2,32,256]{3,2,1,0:T(8,128)(2,1)} collective-permute-done((bf16[12,2,32,256]{3,2,1,0:T(8,128)(2,1)}, bf16[12,2,32,256]{3,2,1,0:T(8,128)(2,1)}, u32[]{:S(2)}, u32[]{:S(2)}) %collective-permute-start.3) | collective-permute-done | bytes 393248 | tf_op jit(solution)/shard_map/ppermute | solution.py:31
  251.3 0.0 collective-permute-start.5
  251.3 1.0 constant_dynamic-update-slice_fusion.5
  252.3 4.0 %collective-permute-done.4 = bf16[12,2,32,256]{3,2,1,0:T(8,128)(2,1)S(1)} collective-permute-done((bf16[12,2,32,256]{3,2,1,0:T(8,128)(2,1)}, bf16[12,2,32,256]{3,2,1,0:T(8,128)(2,1)S(1)}, u32[]{:S(2)}, u32[]{:S(2)}) %collective-permute-start.4) | collective-permute-done | bytes 393248 | tf_op jit(solution)/shard_map/ppermute | solution.py:28
  256.4 0.9 collective-permute-start.6
  257.2 1.0 constant_dynamic-update-slice_fusion.4
  258.3 1.0 constant_dynamic-update-slice_fusion.3
  259.3 15.2 %collective-permute-done.5 = bf16[12,2,32,256]{3,2,1,0:T(8,128)(2,1)S(1)} collective-permute-done((bf16[12,2,32,256]{3,2,1,0:T(8,128)(2,1)}, bf16[12,2,32,256]{3,2,1,0:T(8,128)(2,1)S(1)}, u32[]{:S(2)}, u32[]{:S(2)}) %collective-permute-start.5) | collective-permute-done | bytes 393248 | tf_op jit(solution)/shard_map/ppermute | solution.py:31
  274.6 8.1 %collective-permute-done.6 = bf16[12,2,32,256]{3,2,1,0:T(8,128)(2,1)S(1)} collective-permute-done((bf16[12,2,32,256]{3,2,1,0:T(8,128)(2,1)S(1)}, bf16[12,2,32,256]{3,2,1,0:T(8,128)(2,1)S(1)}, u32[]{:S(2)}, u32[]{:S(2)}) %collective-permute-start.6) | collective-permute-done | bytes 393248 | tf_op jit(solution)/shard_map/ppermute | solution.py:28
  282.7 0.0 copy-start
  282.7 0.0 all-gather.2.cloned.1.call-done
  282.7 5.0 %copy.21 = bf16[12,2,256,256]{3,2,1,0:T(8,128)(2,1)} copy(bf16[12,2,256,256]{3,2,1,0:T(8,128)(2,1)} %all-gather.2.cloned.1.call-done) | data formatting | bytes 6291456
  287.7 0.0 copy-done
  (3 shorter events, 0.1 us)
Async XLA Ops:
  7.2 126.7 %reduce-scatter.2.cloned.1.call-start = ((), (), s32[]{:S(2)}) async-start(), calls=%async_computation.1 | async-start | bytes 7077888 | tf_op jit(solution)/shard_map/reduce_scatter | solution.py:41
  12.5 163.8 %copy-start.2 = (f32[12,2,32,256]{3,2,1,0:T(8,128)S(1)}, f32[12,2,32,256]{3,2,1,0:T(8,128)}, u32[]{:S(2)}) copy-start(f32[12,2,32,256]{3,2,1,0:T(8,128)} %param.8) | copy-start | bytes 2359300
  12.5 163.8 %copy-start.3 = (f32[12,2,32,256]{3,2,1,0:T(8,128)S(1)}, f32[12,2,32,256]{3,2,1,0:T(8,128)}, u32[]{:S(2)}) copy-start(f32[12,2,32,256]{3,2,1,0:T(8,128)} %param.7) | copy-start | bytes 2359300
  12.5 163.8 %copy-start.4 = (f32[12,2,32,256]{3,2,1,0:T(8,128)S(1)}, f32[12,2,32,256]{3,2,1,0:T(8,128)}, u32[]{:S(2)}) copy-start(f32[12,2,32,256]{3,2,1,0:T(8,128)} %param.9) | copy-start | bytes 2359300
  12.5 163.8 %copy-start.5 = (f32[12,2,32,256]{3,2,1,0:T(8,128)S(1)}, f32[12,2,32,256]{3,2,1,0:T(8,128)}, u32[]{:S(2)}) copy-start(f32[12,2,32,256]{3,2,1,0:T(8,128)} %param.10) | copy-start | bytes 2359300
  12.5 163.8 %copy-start.7 = (f32[12]{0:T(128)S(1)}, f32[12]{0:T(128)}, u32[]{:S(2)}) copy-start(f32[12]{0:T(128)} %param.11) | copy-start | bytes 148
  12.6 270.1 %all-gather.2.cloned.1.call-start = ((), (), s32[]{:S(2)}) async-start(), calls=%async_computation.2 | async-start | bytes 3538944 | tf_op jit(solution)/shard_map/all_gather | solution.py:56
  179.9 1.1 copy-start.1
  181.1 16.9 %collective-permute-start = (bf16[12,2,32,256]{3,2,1,0:T(8,128)(2,1)S(1)}, bf16[12,2,32,256]{3,2,1,0:T(8,128)(2,1)S(1)}, u32[]{:S(2)}, u32[]{:S(2)}) collective-permute-start(bf16[12,2,32,256]{3,2,1,0:T(8,128)(2,1)S(1)} %get-tuple-element.12), channel_id=1, source_target_pairs={{0,4},{4,8},{8,12},{12,16},{16,20},{20,24},{24,28},{28,0},{1,5},{5... | collective-permute-start | bytes 1179656 | tf_op jit(solution)/shard_map/ppermute | solution.py:28
  182.2 35.2 %collective-permute-start.1 = (bf16[12,2,32,256]{3,2,1,0:T(8,128)(2,1)S(1)}, bf16[12,2,32,256]{3,2,1,0:T(8,128)(2,1)}, u32[]{:S(2)}, u32[]{:S(2)}) collective-permute-start(bf16[12,2,32,256]{3,2,1,0:T(8,128)(2,1)S(1)} %get-tuple-element.12), channel_id=1, source_target_pairs={{0,28},{4,0},{8,4},{12,8},{16,12},{20,16},{24,20},{28,24},{1,29},{... | collective-permute-start | bytes 1179656 | tf_op jit(solution)/shard_map/ppermute | solution.py:31
  198.0 19.4 %copy-start.6 = (bf16[12,2,32,256]{3,2,1,0:T(8,128)(2,1)}, bf16[12,2,32,256]{3,2,1,0:T(8,128)(2,1)S(1)}, u32[]{:S(2)}) copy-start(bf16[12,2,32,256]{3,2,1,0:T(8,128)(2,1)S(1)} %collective-permute-done) | copy-start | bytes 1179652
  198.0 27.4 %collective-permute-start.2 = (bf16[12,2,32,256]{3,2,1,0:T(8,128)(2,1)S(1)}, bf16[12,2,32,256]{3,2,1,0:T(8,128)(2,1)}, u32[]{:S(2)}, u32[]{:S(2)}) collective-permute-start(bf16[12,2,32,256]{3,2,1,0:T(8,128)(2,1)S(1)} %collective-permute-done), channel_id=1, source_target_pairs={{0,4},{4,8},{8,12},{12,16},{16,20},{20,24},{24,28},{28,0},{1,5},{5... | collective-permute-start | bytes 1179656 | tf_op jit(solution)/shard_map/ppermute | solution.py:28
  217.4 33.9 %collective-permute-start.3 = (bf16[12,2,32,256]{3,2,1,0:T(8,128)(2,1)}, bf16[12,2,32,256]{3,2,1,0:T(8,128)(2,1)}, u32[]{:S(2)}, u32[]{:S(2)}) collective-permute-start(bf16[12,2,32,256]{3,2,1,0:T(8,128)(2,1)} %collective-permute-done.1), channel_id=1, source_target_pairs={{0,28},{4,0},{8,4},{12,8},{16,12},{20,16},{24,20},{28,24},{1,29},{... | collective-permute-start | bytes 1179656 | tf_op jit(solution)/shard_map/ppermute | solution.py:31
  225.5 30.9 %collective-permute-start.4 = (bf16[12,2,32,256]{3,2,1,0:T(8,128)(2,1)}, bf16[12,2,32,256]{3,2,1,0:T(8,128)(2,1)S(1)}, u32[]{:S(2)}, u32[]{:S(2)}) collective-permute-start(bf16[12,2,32,256]{3,2,1,0:T(8,128)(2,1)} %collective-permute-done.2), channel_id=1, source_target_pairs={{0,4},{4,8},{8,12},{12,16},{16,20},{20,24},{24,28},{28,0},{1,5},{5... | collective-permute-start | bytes 1179656 | tf_op jit(solution)/shard_map/ppermute | solution.py:28
  251.3 23.2 %collective-permute-start.5 = (bf16[12,2,32,256]{3,2,1,0:T(8,128)(2,1)}, bf16[12,2,32,256]{3,2,1,0:T(8,128)(2,1)S(1)}, u32[]{:S(2)}, u32[]{:S(2)}) collective-permute-start(bf16[12,2,32,256]{3,2,1,0:T(8,128)(2,1)} %collective-permute-done.3), channel_id=1, source_target_pairs={{0,28},{4,0},{8,4},{12,8},{16,12},{20,16},{24,20},{28,24},{1,29},{... | collective-permute-start | bytes 1179656 | tf_op jit(solution)/shard_map/ppermute | solution.py:31
  256.4 26.2 %collective-permute-start.6 = (bf16[12,2,32,256]{3,2,1,0:T(8,128)(2,1)S(1)}, bf16[12,2,32,256]{3,2,1,0:T(8,128)(2,1)S(1)}, u32[]{:S(2)}, u32[]{:S(2)}) collective-permute-start(bf16[12,2,32,256]{3,2,1,0:T(8,128)(2,1)S(1)} %collective-permute-done.4), channel_id=1, source_target_pairs={{0,4},{4,8},{8,12},{12,16},{16,20},{20,24},{24,28},{28,0},{1,5},{5... | collective-permute-start | bytes 1179656 | tf_op jit(solution)/shard_map/ppermute | solution.py:28
  282.7 5.0 %copy-start = (bf16[12,2,256,256]{3,2,1,0:T(8,128)(2,1)}, bf16[12,2,256,256]{3,2,1,0:T(8,128)(2,1)S(1)}, u32[]{:S(2)}) copy-start(bf16[12,2,256,256]{3,2,1,0:T(8,128)(2,1)S(1)} %constant_dynamic-update-slice_fusion) | copy-start | bytes 9437188
Sparse Core Ops, SparseCore 0:
  12.7 121.1 reduce-scatter.1
  180.0 93.7 all-gather.1
